TPU v7x, 8 devices: a whole 2x2x1 slice. The times are simulated.
8 devices in a mesh: batch: 1 (over z), gz: 2 (over y), gy: 2 (over x), gx: 2 (over core).
Axes of the slice: x: 2, y: 2, z: 1, core: 2. Of those that a mesh axis runs over, the one named last changes fastest.
Arguments:
- u_init: float32 [64, 128, 128], P(('batch', 'gx'), 'gy', 'gz')
- f_rhs: float32 [64, 128, 128], P(('batch', 'gx'), 'gy', 'gz')
- kappa_cell: float32 [64, 128, 128], P(('batch', 'gx'), 'gy', 'gz')
- stencil_w: float32 [26], replicated
- omega_sweep: float32 [32], replicated
Outputs:
- output: float32 [64, 128, 128], P(('batch', 'gx'), 'gy', 'gz')
All inputs are finite; a program needn't handle non-finite values.
Results may differ from a plain program's by a relative error of at most 0.001.
Values are sent between devices in bfloat16 or wider.
A program may use at most 1 GiB of HBM per device.

v0:
```python
import jax
import jax.numpy as jnp
from jax import lax
from jax.sharding import PartitionSpec as P, NamedSharding

MESH_AXES = ("gx", "gy", "gz")


def offset_list():
    unit_steps = (-1, 0, 1)
    return [(a, b, c) for a in unit_steps for b in unit_steps for c in unit_steps if (a, b, c) != (0, 0, 0)]


def window(array_in, offset, out_shape):
    lo_x = 1 + offset[0]
    lo_y = 1 + offset[1]
    lo_z = 1 + offset[2]
    return array_in[..., lo_x:lo_x + out_shape[0], lo_y:lo_y + out_shape[1], lo_z:lo_z + out_shape[2]]


def diag_sum(kappa_ext, stencil_w, out_shape):
    k_mid = window(kappa_ext, (0, 0, 0), out_shape)
    diag_total = jnp.zeros_like(k_mid)
    for w_idx, offset in enumerate(offset_list()):
        diag_total = diag_total + stencil_w[w_idx] * (0.5 * (k_mid + window(kappa_ext, offset, out_shape)))
    return diag_total


def jacobi_step(u_ext, kappa_ext, f_reg, diag_reg, stencil_w, relax_now):
    out_shape = f_reg.shape[-3:]
    u_mid = window(u_ext, (0, 0, 0), out_shape)
    k_mid = window(kappa_ext, (0, 0, 0), out_shape)
    applied = jnp.zeros_like(u_mid)
    for w_idx, offset in enumerate(offset_list()):
        coef_io = stencil_w[w_idx] * (0.5 * (k_mid + window(kappa_ext, offset, out_shape)))
        applied = applied + coef_io * (u_mid - window(u_ext, offset, out_shape))
    return u_mid + relax_now * (f_reg - applied) / diag_reg


def halo_axis(brick_in, axis_name, axis_size, axis_dim, halo_depth):
    extent = brick_in.shape[axis_dim]
    low_part = lax.slice_in_dim(brick_in, 0, halo_depth, axis=axis_dim)
    high_part = lax.slice_in_dim(brick_in, extent - halo_depth, extent, axis=axis_dim)
    to_next = [(source_idx, (source_idx + 1) % axis_size) for source_idx in range(axis_size)]
    to_prev = [(source_idx, (source_idx - 1) % axis_size) for source_idx in range(axis_size)]
    from_prev = lax.ppermute(high_part, axis_name, to_next)
    from_next = lax.ppermute(low_part, axis_name, to_prev)
    return jnp.concatenate([from_prev, brick_in, from_next], axis=axis_dim)


def halo_all(brick_in, axis_sizes, halo_depth):
    padded = brick_in
    for axis_dim, axis_name in enumerate(MESH_AXES):
        padded = halo_axis(padded, axis_name, axis_sizes[axis_dim], axis_dim, halo_depth)
    return padded


def solution(mesh):
    axis_sizes = tuple(mesh.shape[axis_name] for axis_name in MESH_AXES)
    brick_spec = P(("batch", "gx"), "gy", "gz")

    def local_sweeps(u_brick, f_brick, kappa_brick, stencil_w, omega_sweep):
        kappa_ext = halo_all(kappa_brick, axis_sizes, 1)
        diag_brick = diag_sum(kappa_ext, stencil_w, f_brick.shape)

        def sweep_body(sweep_idx, u_now):
            u_ext = halo_all(u_now, axis_sizes, 1)
            return jacobi_step(u_ext, kappa_ext, f_brick, diag_brick, stencil_w, omega_sweep[sweep_idx])

        return lax.fori_loop(0, omega_sweep.shape[0], sweep_body, u_brick)

    return jax.shard_map(local_sweeps, mesh=mesh, in_specs=(brick_spec, brick_spec, brick_spec, P(), P()), out_specs=brick_spec, check_vma=False)
```

profile of v0, /device:TPU:0, one launch (start us, length us, event | category | flops | bytes accessed | tf_op | source)
XLA Modules:
  0.0 1260.2 jit_solution(9903571890042285096)
XLA Ops:
  55.0 1205.1 %while.15 = (s32[]{:T(128)}, f32[32,64,64]{2,1,0:T(8,128)}, f32[32]{0:T(128)}, f32[]{:T(128)}, f32[32,64,64]{2,1,0:T(8,128)}, /*index=5*/f32[]{:T(128)}, f32[32,...) while((s32[]{:T(128)}, f32[32,64,64]{2,1,0:T(8,128)}, ...), condition=%wide.region_1.0_spmd, body=%wide.region_0.0_spmd.sunk | while | flops 16235674 | bytes 34852724 | solution.py:70
  75.3 17.3 %divide_add_fusion.2 = f32[32,64,64]{2,1,0:T(8,128)} fusion(f32[32,64,64]{2,1,0:T(8,128)S(1)} %copy.71, f32[32,64,64]{2,1,0:T(8,128)} %get-tuple-element.1253, f32[32,64,64]{2,1,0:T(8,128)} %get-tuple-element.1252, f32[34,66,65]{2,1,0:T(8,128)S(1)} %get-tuple-element.1079, f32[32,64,64]{2,1,0:T(8,128)} %get-tuple-element.1251, ...), kind=kLoop, calls=%fused_computation.97.clone.1 | loop fusion | flops 15073280 | bytes 25773164 | tf_op jit(solution)/shard_map/while/body/eval_jaxpr/add | solution.py:37
  113.4 17.3 %divide_add_fusion.2 = f32[32,64,64]{2,1,0:T(8,128)} fusion(f32[32,64,64]{2,1,0:T(8,128)S(1)} %copy.71, f32[32,64,64]{2,1,0:T(8,128)} %get-tuple-element.1253, f32[32,64,64]{2,1,0:T(8,128)} %get-tuple-element.1252, f32[34,66,65]{2,1,0:T(8,128)S(1)} %get-tuple-element.1079, f32[32,64,64]{2,1,0:T(8,128)} %get-tuple-element.1251, ...), kind=kLoop, calls=%fused_computation.97.clone.1 | loop fusion | flops 15073280 | bytes 25773164 | tf_op jit(solution)/shard_map/while/body/eval_jaxpr/add | solution.py:37
  150.6 17.3 %divide_add_fusion.2 = f32[32,64,64]{2,1,0:T(8,128)} fusion(f32[32,64,64]{2,1,0:T(8,128)S(1)} %copy.71, f32[32,64,64]{2,1,0:T(8,128)} %get-tuple-element.1253, f32[32,64,64]{2,1,0:T(8,128)} %get-tuple-element.1252, f32[34,66,65]{2,1,0:T(8,128)S(1)} %get-tuple-element.1079, f32[32,64,64]{2,1,0:T(8,128)} %get-tuple-element.1251, ...), kind=kLoop, calls=%fused_computation.97.clone.1 | loop fusion | flops 15073280 | bytes 25773164 | tf_op jit(solution)/shard_map/while/body/eval_jaxpr/add | solution.py:37
  188.7 17.3 %divide_add_fusion.2 = f32[32,64,64]{2,1,0:T(8,128)} fusion(f32[32,64,64]{2,1,0:T(8,128)S(1)} %copy.71, f32[32,64,64]{2,1,0:T(8,128)} %get-tuple-element.1253, f32[32,64,64]{2,1,0:T(8,128)} %get-tuple-element.1252, f32[34,66,65]{2,1,0:T(8,128)S(1)} %get-tuple-element.1079, f32[32,64,64]{2,1,0:T(8,128)} %get-tuple-element.1251, ...), kind=kLoop, calls=%fused_computation.97.clone.1 | loop fusion | flops 15073280 | bytes 25773164 | tf_op jit(solution)/shard_map/while/body/eval_jaxpr/add | solution.py:37
  225.9 17.3 %divide_add_fusion.2 = f32[32,64,64]{2,1,0:T(8,128)} fusion(f32[32,64,64]{2,1,0:T(8,128)S(1)} %copy.71, f32[32,64,64]{2,1,0:T(8,128)} %get-tuple-element.1253, f32[32,64,64]{2,1,0:T(8,128)} %get-tuple-element.1252, f32[34,66,65]{2,1,0:T(8,128)S(1)} %get-tuple-element.1079, f32[32,64,64]{2,1,0:T(8,128)} %get-tuple-element.1251, ...), kind=kLoop, calls=%fused_computation.97.clone.1 | loop fusion | flops 15073280 | bytes 25773164 | tf_op jit(solution)/shard_map/while/body/eval_jaxpr/add | solution.py:37
  264.0 17.3 %divide_add_fusion.2 = f32[32,64,64]{2,1,0:T(8,128)} fusion(f32[32,64,64]{2,1,0:T(8,128)S(1)} %copy.71, f32[32,64,64]{2,1,0:T(8,128)} %get-tuple-element.1253, f32[32,64,64]{2,1,0:T(8,128)} %get-tuple-element.1252, f32[34,66,65]{2,1,0:T(8,128)S(1)} %get-tuple-element.1079, f32[32,64,64]{2,1,0:T(8,128)} %get-tuple-element.1251, ...), kind=kLoop, calls=%fused_computation.97.clone.1 | loop fusion | flops 15073280 | bytes 25773164 | tf_op jit(solution)/shard_map/while/body/eval_jaxpr/add | solution.py:37
  301.2 17.3 %divide_add_fusion.2 = f32[32,64,64]{2,1,0:T(8,128)} fusion(f32[32,64,64]{2,1,0:T(8,128)S(1)} %copy.71, f32[32,64,64]{2,1,0:T(8,128)} %get-tuple-element.1253, f32[32,64,64]{2,1,0:T(8,128)} %get-tuple-element.1252, f32[34,66,65]{2,1,0:T(8,128)S(1)} %get-tuple-element.1079, f32[32,64,64]{2,1,0:T(8,128)} %get-tuple-element.1251, ...), kind=kLoop, calls=%fused_computation.97.clone.1 | loop fusion | flops 15073280 | bytes 25773164 | tf_op jit(solution)/shard_map/while/body/eval_jaxpr/add | solution.py:37
  339.3 17.3 %divide_add_fusion.2 = f32[32,64,64]{2,1,0:T(8,128)} fusion(f32[32,64,64]{2,1,0:T(8,128)S(1)} %copy.71, f32[32,64,64]{2,1,0:T(8,128)} %get-tuple-element.1253, f32[32,64,64]{2,1,0:T(8,128)} %get-tuple-element.1252, f32[34,66,65]{2,1,0:T(8,128)S(1)} %get-tuple-element.1079, f32[32,64,64]{2,1,0:T(8,128)} %get-tuple-element.1251, ...), kind=kLoop, calls=%fused_computation.97.clone.1 | loop fusion | flops 15073280 | bytes 25773164 | tf_op jit(solution)/shard_map/while/body/eval_jaxpr/add | solution.py:37
  376.5 17.3 %divide_add_fusion.2 = f32[32,64,64]{2,1,0:T(8,128)} fusion(f32[32,64,64]{2,1,0:T(8,128)S(1)} %copy.71, f32[32,64,64]{2,1,0:T(8,128)} %get-tuple-element.1253, f32[32,64,64]{2,1,0:T(8,128)} %get-tuple-element.1252, f32[34,66,65]{2,1,0:T(8,128)S(1)} %get-tuple-element.1079, f32[32,64,64]{2,1,0:T(8,128)} %get-tuple-element.1251, ...), kind=kLoop, calls=%fused_computation.97.clone.1 | loop fusion | flops 15073280 | bytes 25773164 | tf_op jit(solution)/shard_map/while/body/eval_jaxpr/add | solution.py:37
  414.6 17.3 %divide_add_fusion.2 = f32[32,64,64]{2,1,0:T(8,128)} fusion(f32[32,64,64]{2,1,0:T(8,128)S(1)} %copy.71, f32[32,64,64]{2,1,0:T(8,128)} %get-tuple-element.1253, f32[32,64,64]{2,1,0:T(8,128)} %get-tuple-element.1252, f32[34,66,65]{2,1,0:T(8,128)S(1)} %get-tuple-element.1079, f32[32,64,64]{2,1,0:T(8,128)} %get-tuple-element.1251, ...), kind=kLoop, calls=%fused_computation.97.clone.1 | loop fusion | flops 15073280 | bytes 25773164 | tf_op jit(solution)/shard_map/while/body/eval_jaxpr/add | solution.py:37
  451.8 17.3 %divide_add_fusion.2 = f32[32,64,64]{2,1,0:T(8,128)} fusion(f32[32,64,64]{2,1,0:T(8,128)S(1)} %copy.71, f32[32,64,64]{2,1,0:T(8,128)} %get-tuple-element.1253, f32[32,64,64]{2,1,0:T(8,128)} %get-tuple-element.1252, f32[34,66,65]{2,1,0:T(8,128)S(1)} %get-tuple-element.1079, f32[32,64,64]{2,1,0:T(8,128)} %get-tuple-element.1251, ...), kind=kLoop, calls=%fused_computation.97.clone.1 | loop fusion | flops 15073280 | bytes 25773164 | tf_op jit(solution)/shard_map/while/body/eval_jaxpr/add | solution.py:37
  489.9 17.3 %divide_add_fusion.2 = f32[32,64,64]{2,1,0:T(8,128)} fusion(f32[32,64,64]{2,1,0:T(8,128)S(1)} %copy.71, f32[32,64,64]{2,1,0:T(8,128)} %get-tuple-element.1253, f32[32,64,64]{2,1,0:T(8,128)} %get-tuple-element.1252, f32[34,66,65]{2,1,0:T(8,128)S(1)} %get-tuple-element.1079, f32[32,64,64]{2,1,0:T(8,128)} %get-tuple-element.1251, ...), kind=kLoop, calls=%fused_computation.97.clone.1 | loop fusion | flops 15073280 | bytes 25773164 | tf_op jit(solution)/shard_map/while/body/eval_jaxpr/add | solution.py:37
  527.1 17.3 %divide_add_fusion.2 = f32[32,64,64]{2,1,0:T(8,128)} fusion(f32[32,64,64]{2,1,0:T(8,128)S(1)} %copy.71, f32[32,64,64]{2,1,0:T(8,128)} %get-tuple-element.1253, f32[32,64,64]{2,1,0:T(8,128)} %get-tuple-element.1252, f32[34,66,65]{2,1,0:T(8,128)S(1)} %get-tuple-element.1079, f32[32,64,64]{2,1,0:T(8,128)} %get-tuple-element.1251, ...), kind=kLoop, calls=%fused_computation.97.clone.1 | loop fusion | flops 15073280 | bytes 25773164 | tf_op jit(solution)/shard_map/while/body/eval_jaxpr/add | solution.py:37
  565.1 17.3 %divide_add_fusion.2 = f32[32,64,64]{2,1,0:T(8,128)} fusion(f32[32,64,64]{2,1,0:T(8,128)S(1)} %copy.71, f32[32,64,64]{2,1,0:T(8,128)} %get-tuple-element.1253, f32[32,64,64]{2,1,0:T(8,128)} %get-tuple-element.1252, f32[34,66,65]{2,1,0:T(8,128)S(1)} %get-tuple-element.1079, f32[32,64,64]{2,1,0:T(8,128)} %get-tuple-element.1251, ...), kind=kLoop, calls=%fused_computation.97.clone.1 | loop fusion | flops 15073280 | bytes 25773164 | tf_op jit(solution)/shard_map/while/body/eval_jaxpr/add | solution.py:37
  602.4 17.3 %divide_add_fusion.2 = f32[32,64,64]{2,1,0:T(8,128)} fusion(f32[32,64,64]{2,1,0:T(8,128)S(1)} %copy.71, f32[32,64,64]{2,1,0:T(8,128)} %get-tuple-element.1253, f32[32,64,64]{2,1,0:T(8,128)} %get-tuple-element.1252, f32[34,66,65]{2,1,0:T(8,128)S(1)} %get-tuple-element.1079, f32[32,64,64]{2,1,0:T(8,128)} %get-tuple-element.1251, ...), kind=kLoop, calls=%fused_computation.97.clone.1 | loop fusion | flops 15073280 | bytes 25773164 | tf_op jit(solution)/shard_map/while/body/eval_jaxpr/add | solution.py:37
  640.4 17.3 %divide_add_fusion.2 = f32[32,64,64]{2,1,0:T(8,128)} fusion(f32[32,64,64]{2,1,0:T(8,128)S(1)} %copy.71, f32[32,64,64]{2,1,0:T(8,128)} %get-tuple-element.1253, f32[32,64,64]{2,1,0:T(8,128)} %get-tuple-element.1252, f32[34,66,65]{2,1,0:T(8,128)S(1)} %get-tuple-element.1079, f32[32,64,64]{2,1,0:T(8,128)} %get-tuple-element.1251, ...), kind=kLoop, calls=%fused_computation.97.clone.1 | loop fusion | flops 15073280 | bytes 25773164 | tf_op jit(solution)/shard_map/while/body/eval_jaxpr/add | solution.py:37
  677.7 17.3 %divide_add_fusion.2 = f32[32,64,64]{2,1,0:T(8,128)} fusion(f32[32,64,64]{2,1,0:T(8,128)S(1)} %copy.71, f32[32,64,64]{2,1,0:T(8,128)} %get-tuple-element.1253, f32[32,64,64]{2,1,0:T(8,128)} %get-tuple-element.1252, f32[34,66,65]{2,1,0:T(8,128)S(1)} %get-tuple-element.1079, f32[32,64,64]{2,1,0:T(8,128)} %get-tuple-element.1251, ...), kind=kLoop, calls=%fused_computation.97.clone.1 | loop fusion | flops 15073280 | bytes 25773164 | tf_op jit(solution)/shard_map/while/body/eval_jaxpr/add | solution.py:37
  715.7 17.3 %divide_add_fusion.2 = f32[32,64,64]{2,1,0:T(8,128)} fusion(f32[32,64,64]{2,1,0:T(8,128)S(1)} %copy.71, f32[32,64,64]{2,1,0:T(8,128)} %get-tuple-element.1253, f32[32,64,64]{2,1,0:T(8,128)} %get-tuple-element.1252, f32[34,66,65]{2,1,0:T(8,128)S(1)} %get-tuple-element.1079, f32[32,64,64]{2,1,0:T(8,128)} %get-tuple-element.1251, ...), kind=kLoop, calls=%fused_computation.97.clone.1 | loop fusion | flops 15073280 | bytes 25773164 | tf_op jit(solution)/shard_map/while/body/eval_jaxpr/add | solution.py:37
  753.0 17.3 %divide_add_fusion.2 = f32[32,64,64]{2,1,0:T(8,128)} fusion(f32[32,64,64]{2,1,0:T(8,128)S(1)} %copy.71, f32[32,64,64]{2,1,0:T(8,128)} %get-tuple-element.1253, f32[32,64,64]{2,1,0:T(8,128)} %get-tuple-element.1252, f32[34,66,65]{2,1,0:T(8,128)S(1)} %get-tuple-element.1079, f32[32,64,64]{2,1,0:T(8,128)} %get-tuple-element.1251, ...), kind=kLoop, calls=%fused_computation.97.clone.1 | loop fusion | flops 15073280 | bytes 25773164 | tf_op jit(solution)/shard_map/while/body/eval_jaxpr/add | solution.py:37
  1016.9 17.3 %divide_add_fusion.2 = f32[32,64,64]{2,1,0:T(8,128)} fusion(f32[32,64,64]{2,1,0:T(8,128)S(1)} %copy.71, f32[32,64,64]{2,1,0:T(8,128)} %get-tuple-element.1253, f32[32,64,64]{2,1,0:T(8,128)} %get-tuple-element.1252, f32[34,66,65]{2,1,0:T(8,128)S(1)} %get-tuple-element.1079, f32[32,64,64]{2,1,0:T(8,128)} %get-tuple-element.1251, ...), kind=kLoop, calls=%fused_computation.97.clone.1 | loop fusion | flops 15073280 | bytes 25773164 | tf_op jit(solution)/shard_map/while/body/eval_jaxpr/add | solution.py:37
  1092.2 17.3 %divide_add_fusion.2 = f32[32,64,64]{2,1,0:T(8,128)} fusion(f32[32,64,64]{2,1,0:T(8,128)S(1)} %copy.71, f32[32,64,64]{2,1,0:T(8,128)} %get-tuple-element.1253, f32[32,64,64]{2,1,0:T(8,128)} %get-tuple-element.1252, f32[34,66,65]{2,1,0:T(8,128)S(1)} %get-tuple-element.1079, f32[32,64,64]{2,1,0:T(8,128)} %get-tuple-element.1251, ...), kind=kLoop, calls=%fused_computation.97.clone.1 | loop fusion | flops 15073280 | bytes 25773164 | tf_op jit(solution)/shard_map/while/body/eval_jaxpr/add | solution.py:37
  1167.5 17.3 %divide_add_fusion.2 = f32[32,64,64]{2,1,0:T(8,128)} fusion(f32[32,64,64]{2,1,0:T(8,128)S(1)} %copy.71, f32[32,64,64]{2,1,0:T(8,128)} %get-tuple-element.1253, f32[32,64,64]{2,1,0:T(8,128)} %get-tuple-element.1252, f32[34,66,65]{2,1,0:T(8,128)S(1)} %get-tuple-element.1079, f32[32,64,64]{2,1,0:T(8,128)} %get-tuple-element.1251, ...), kind=kLoop, calls=%fused_computation.97.clone.1 | loop fusion | flops 15073280 | bytes 25773164 | tf_op jit(solution)/shard_map/while/body/eval_jaxpr/add | solution.py:37
  1242.8 17.3 %divide_add_fusion.2 = f32[32,64,64]{2,1,0:T(8,128)} fusion(f32[32,64,64]{2,1,0:T(8,128)S(1)} %copy.71, f32[32,64,64]{2,1,0:T(8,128)} %get-tuple-element.1253, f32[32,64,64]{2,1,0:T(8,128)} %get-tuple-element.1252, f32[34,66,65]{2,1,0:T(8,128)S(1)} %get-tuple-element.1079, f32[32,64,64]{2,1,0:T(8,128)} %get-tuple-element.1251, ...), kind=kLoop, calls=%fused_computation.97.clone.1 | loop fusion | flops 15073280 | bytes 25773164 | tf_op jit(solution)/shard_map/while/body/eval_jaxpr/add | solution.py:37
  (1269 shorter events, 843.2 us)
Async XLA Ops:
  4.5 4.4 collective-permute-start.8
  13.2 19.3 %collective-permute-start.10 = (f32[34,66,1]{1,2,0:T(1,128)}, f32[34,66,1]{1,2,0:T(1,128)S(1)}, u32[]{:S(2)}, u32[]{:S(2)}) collective-permute-start(f32[34,66,1]{1,2,0:T(1,128)} %copy.44), channel_id=1, source_target_pairs={{0,4},{4,0},{1,5},{5,1},{2,6},{6,2},{3,7},{7,3}} | collective-permute-start | bytes 26936 | tf_op jit(solution)/shard_map/ppermute | solution.py:46
  15.2 18.9 %collective-permute-start.11 = (f32[34,66,1]{1,2,0:T(1,128)S(1)}, f32[34,66,1]{1,2,0:T(1,128)S(1)}, u32[]{:S(2)}, u32[]{:S(2)}) collective-permute-start(f32[34,66,1]{1,2,0:T(1,128)S(1)} %copy.46), channel_id=1, source_target_pairs={{0,4},{4,0},{1,5},{5,1},{2,6},{6,2},{3,7},{7,3}} | collective-permute-start | bytes 26936 | tf_op jit(solution)/shard_map/ppermute | solution.py:47
  133.9 3.8 collective-permute-start.2
  209.2 3.8 collective-permute-start.2
  246.4 3.8 collective-permute-start.2
  284.5 3.8 collective-permute-start.2
  321.7 3.8 collective-permute-start.2
  359.8 3.8 collective-permute-start.2
  397.0 3.8 collective-permute-start.2
  472.3 3.8 collective-permute-start.2
  547.6 3.8 collective-permute-start.2
  622.9 3.8 collective-permute-start.2
  736.3 3.8 collective-permute-start.2
  811.6 3.8 collective-permute-start.2
  886.9 3.8 collective-permute-start.2
  924.1 3.8 collective-permute-start.2
  962.1 3.8 collective-permute-start.2
  999.4 3.8 collective-permute-start.2
  1037.4 3.8 collective-permute-start.2
  1074.7 3.8 collective-permute-start.2
  1112.7 3.8 collective-permute-start.2
  1150.0 3.8 collective-permute-start.2
  1225.3 3.8 collective-permute-start.2
  (374 other events, 965.5 us)
where the time goes:
time: 1260 us
  other arithmetic  680 us (54%)
  local copies, waits for them, and re-layouts  273 us (22%)
  starting transfers between devices  153 us (12%)
  waiting for transfers between devices  135 us (11%)
  between operations  16.3 us (1%)
    add x32, other arithmetic, jacobi_step(): return u_mid + relax_now * (f_reg - applied) / diag_reg  553 us
    concatenate x66, other arithmetic, halo_axis(): return jnp.concatenate([from_prev, brick_in, from_next], axis=axis_dim)  111 us
    while x480, local copies, waits for them, and re-layouts  81.7 us
    ppermute x99, starting transfers between devices, halo_axis(): from_next = lax.ppermute(low_part, axis_name, to_prev)  79.7 us
    ppermute x99, waiting for transfers between devices, halo_axis(): from_prev = lax.ppermute(high_part, axis_name, to_next)  76.8 us
    ppermute x99, starting transfers between devices, halo_axis(): from_prev = lax.ppermute(high_part, axis_name, to_next)  73 us
    ppermute x99, waiting for transfers between devices, halo_axis(): from_next = lax.ppermute(low_part, axis_name, to_prev)  58 us
    ppermute x33, local copies, waits for them, and re-layouts, halo_axis(): from_prev = lax.ppermute(high_part, axis_name, to_next)  51.6 us
  transfers between devices with their start and end apart: 198, of which 133 were waited for; matrix products, arithmetic and copies ran while one was open for 7% of the time, Pallas kernels for 0%

commit v1 on v0

v1 whole, which is shorter than its diff:
```python
import functools

import jax
import jax.numpy as jnp
from jax import lax
from jax.experimental import pallas as pl
from jax.experimental.pallas import tpu as pltpu
from jax.sharding import PartitionSpec as P

MESH = pl.DeviceIdType.MESH
S = 4
ZB = 2
NZ, NU, LANES = 32, 32, 128
PAD = 16
ROWS = 56
ZE = NZ + 2 * S
FOLD = PAD + NU
SCALE = 2.0 ** -9
NCOPY = 2 + 3 * S
OFFSETS = [(a, b, c) for a in (-1, 0, 1) for b in (-1, 0, 1) for c in (-1, 0, 1) if (a, b, c) != (0, 0, 0)]
INDEX = {o: m for m, o in enumerate(OFFSETS)}


def swap_pairs(v, even):
    return jnp.where(even, pltpu.roll(v, LANES - 1, 1), pltpu.roll(v, 1, 1))


def exchange_copies(buf, send_sem, recv_sem, peers):
    low, high, gy, gylow, gyhigh = peers
    body = pl.ds(PAD, NU + 1)
    own = pl.ds(S, NZ)
    first, last = pl.ds(S, S), pl.ds(NZ, S)
    below, above = pl.ds(0, S), pl.ds(S + NZ, S)
    plan = [(first, body, above, body, low), (last, body, below, body, high)]
    for j in range(S):
        src, dst = pl.ds(PAD + j, 1), pl.ds(PAD - 1 - j, 1)
        plan.append((own, src, own, dst, gy))
        plan.append((first, src, above, dst, gylow))
        plan.append((last, src, below, dst, gyhigh))
    return [
        pltpu.make_async_remote_copy(
            src_ref=buf.at[sz, su, :],
            dst_ref=buf.at[dz, du, :],
            send_sem=send_sem.at[n],
            recv_sem=recv_sem.at[n],
            device_id=peer,
            device_id_type=MESH,
        )
        for n, (sz, su, dz, du, peer) in enumerate(plan)
    ]


def rows_loop(n_rows, block):
    full = n_rows // ZB

    def body(i, carry):
        block(i * ZB, ZB)
        return carry

    lax.fori_loop(0, full, body, 0)
    if n_rows % ZB:
        block(full * ZB, n_rows % ZB)


def load_window(ref, z0, count, base):
    return [
        [ref[z0 + dz, pl.ds(base + du, 8), :] for du in (-1, 0, 1)]
        for dz in range(-1, count + 1)
    ]


def kernel(n_sweeps, w_ref, om_ref, u_ref, f_ref, k_ref, o_ref,
           abuf, bbuf, cbuf, kbuf, fbuf, idbuf, tbuf,
           in_sem, send_sem, recv_sem, ksend, krecv, fsend, frecv):
    gz, gy, gx = lax.axis_index("gz"), lax.axis_index("gy"), lax.axis_index("gx")
    other = 1 - gx

    def dev(z, y, x):
        return {"batch": lax.axis_index("batch"), "gz": z, "gy": y, "gx": x}

    z_low, z_high = (gz + 1 - gx) % 2, (gz + gx) % 2
    peers = (dev(z_low, gy, other), dev(z_high, gy, other), dev(gz, 1 - gy, gx),
             dev(z_low, 1 - gy, other), dev(z_high, 1 - gy, other))
    own = (pl.ds(S, NZ), pl.ds(PAD, NU))

    loads = [
        pltpu.make_async_copy(src, dst.at[own[0], own[1], :], in_sem.at[n])
        for n, (src, dst) in enumerate(((k_ref, kbuf), (u_ref, abuf.at[0]), (f_ref, fbuf)))
    ]
    for copy in loads:
        copy.start()
    barrier = pltpu.get_barrier_semaphore()
    for peer in peers:
        pl.semaphore_signal(barrier, inc=1, device_id=peer, device_id_type=MESH)
    pl.semaphore_wait(barrier, len(peers))

    lane = lax.broadcasted_iota(jnp.int32, (8, LANES), 1)
    even = lane % 2 == 0
    upright = lane % 2 == gy

    for copy in loads:
        copy.wait()

    def fold(ref, z0, count):
        def body(i, carry):
            v = swap_pairs(ref[z0 + i, pl.ds(FOLD - 8, 8), :], even)
            ref[z0 + i, pl.ds(FOLD, 1), :] = v[7:8, :]
            return carry
        lax.fori_loop(0, count, body, 0)

    fold(kbuf, S, NZ)
    fold(abuf.at[0], S, NZ)
    fold(fbuf, S, NZ)
    setup = (exchange_copies(kbuf, ksend, krecv, peers)
             + exchange_copies(abuf.at[0], send_sem.at[0], recv_sem.at[0], peers)
             + exchange_copies(fbuf, fsend, frecv, peers))
    for copy in setup:
        copy.start()

    weights = {}
    for (a, b, c), m in INDEX.items():
        plain = w_ref[m] * (0.5 * SCALE)
        if b == 0:
            weights[(a, b, c)] = plain
        else:
            weights[(a, b, c)] = jnp.where(upright, plain, w_ref[INDEX[(a, -b, c)]] * (0.5 * SCALE))

    for copy in setup:
        copy.wait()

    def coef_block(z0, count):
        for k in range(-1, 4):
            base = PAD + 8 * k
            win = load_window(kbuf, z0 + 1, count, base)
            for z in range(count):
                mid = win[z + 1][1]
                moved = {0: mid, 1: pltpu.roll(mid, 2, 1), -1: pltpu.roll(mid, LANES - 2, 1)}
                part = {}
                for o, m in INDEX.items():
                    a, b, c = o
                    t = weights[o] * (moved[a] + win[z + 1 + c][1 + b])
                    tbuf[m, z0 + z, pl.ds(8 * (k + 1), 8), :] = t
                    part[a] = t if a not in part else part[a] + t
                diag = part[0] + pltpu.roll(part[1], LANES - 2, 1) + pltpu.roll(part[-1], 2, 1)
                inv = 1.0 / diag
                idbuf[z0 + z + 1, pl.ds(base, 8), :] = inv
                fbuf[z0 + z + 1, pl.ds(base, 8), :] = fbuf[z0 + z + 1, pl.ds(base, 8), :] * (inv * SCALE)

    rows_loop(ZE - 2, coef_block)

    def sweep(src, dst, step, omega):
        depth = S - step
        blocks = range(-1, 4) if depth else range(0, 4)
        start = S - depth

        def block(z0, count):
            z0 = z0 + start
            for k in blocks:
                base = PAD + 8 * k
                win = load_window(src, z0, count, base)
                for z in range(count):
                    part = {}
                    for (a, b, c), m in INDEX.items():
                        t = tbuf[m, z0 + z - 1, pl.ds(8 * (k + 1), 8), :] * win[z + 1 + c][1 + b]
                        part[a] = t if a not in part else part[a] + t
                    total = part[0] + pltpu.roll(part[1], LANES - 2, 1) + pltpu.roll(part[-1], 2, 1)
                    mid = win[z + 1][1]
                    at = (z0 + z, pl.ds(base, 8), slice(None))
                    new = mid + omega * (total * idbuf[at] + fbuf[at] - mid)
                    dst[at] = new
                    if k == 3:
                        dst[z0 + z, pl.ds(FOLD, 1), :] = swap_pairs(new, even)[7:8, :]

        rows_loop(NZ + 2 * depth, block)

    n_macro = n_sweeps // S

    def macro(e, p):
        for step in range(1, S + 1):
            src = abuf.at[p] if step == 1 else (bbuf if step % 2 == 0 else cbuf)
            dst = abuf.at[1 - p] if step == S else (bbuf if step % 2 == 1 else cbuf)
            sweep(src, dst, step, om_ref[e * S + step - 1])

    def body(e, carry):
        p = e % 2
        macro(e, p)
        copies = exchange_copies(abuf.at[1 - p], send_sem.at[1 - p], recv_sem.at[1 - p], peers)
        for copy in copies:
            copy.start()
        for copy in copies:
            copy.wait()
        return carry

    lax.fori_loop(0, n_macro - 1, body, 0)
    macro(n_macro - 1, (n_macro - 1) % 2)
    done = pltpu.make_async_copy(abuf.at[n_macro % 2, own[0], own[1], :], o_ref, in_sem.at[0])
    done.start()
    done.wait()


def fold_in(brick, gy):
    brick = lax.all_to_all(brick, "gx", split_axis=3, concat_axis=1, tiled=True)
    straight, mirrored = brick[:, :, :NU], brick[:, :, NU:][:, :, ::-1]
    first = jnp.where(gy == 0, straight, mirrored)
    second = jnp.where(gy == 0, mirrored, straight)
    both = jnp.stack([first, second], axis=-1)
    return both.transpose(0, 3, 2, 1, 4).reshape(brick.shape[0], NZ, NU, LANES)


def fold_out(u, gy):
    both = u.reshape(NZ, NU, LANES // 2, 2).transpose(2, 1, 0, 3)
    first, second = both[..., 0], both[..., 1]
    straight = jnp.where(gy == 0, first, second)
    mirrored = jnp.where(gy == 0, second, first)
    brick = jnp.concatenate([straight, mirrored[:, ::-1]], axis=1)
    return lax.all_to_all(brick, "gx", split_axis=0, concat_axis=2, tiled=True)


def solution(mesh):
    brick_spec = P(("batch", "gx"), "gy", "gz")

    def local_sweeps(u_brick, f_brick, kappa_brick, stencil_w, omega_sweep):
        gy = lax.axis_index("gy")
        u, f, k = fold_in(jnp.stack([u_brick, f_brick, kappa_brick]), gy)
        dma = pltpu.SemaphoreType.DMA
        plane = (ZE, ROWS, LANES)
        out = pl.pallas_call(
            functools.partial(kernel, omega_sweep.shape[0]),
            out_shape=jax.ShapeDtypeStruct((NZ, NU, LANES), jnp.float32),
            in_specs=[pl.BlockSpec(memory_space=pltpu.SMEM)] * 2 + [pl.BlockSpec(memory_space=pl.ANY)] * 3,
            out_specs=pl.BlockSpec(memory_space=pl.ANY),
            scratch_shapes=[
                pltpu.VMEM((2,) + plane, jnp.float32),
                pltpu.VMEM(plane, jnp.float32),
                pltpu.VMEM(plane, jnp.float32),
                pltpu.VMEM(plane, jnp.float32),
                pltpu.VMEM(plane, jnp.float32),
                pltpu.VMEM(plane, jnp.float32),
                pltpu.VMEM((26, ZE - 2, 40, LANES), jnp.float32),
                dma((3,)), dma((2, NCOPY)), dma((2, NCOPY)),
                dma((NCOPY,)), dma((NCOPY,)), dma((NCOPY,)), dma((NCOPY,)),
            ],
            compiler_params=pltpu.CompilerParams(
                collective_id=0, has_side_effects=True, vmem_limit_bytes=60 * 2 ** 20
            ),
        )(stencil_w, omega_sweep, u, f, k)
        return fold_out(out, gy)

    return jax.shard_map(local_sweeps, mesh=mesh, in_specs=(brick_spec, brick_spec, brick_spec, P(), P()), out_specs=brick_spec, check_vma=False)
```

time: 1260 us -> 214 us (0.17)
  other arithmetic: 680 us -> 15.6 us
  local copies, waits for them, and re-layouts: 273 us -> 46.9 us
  starting transfers between devices: 153 us -> 3.67 us
  Pallas kernels: 0 us -> 140 us
  waiting for transfers between devices: 135 us -> 2.62 us
  between operations: 16.3 us -> 0.13 us
    add x33 -> x0, other arithmetic: 569 us -> none  [the longest x32 553 us: jacobi_step(): return u_mid + relax_now * (f_reg - applied) / diag_reg]
    ppermute x198 -> x0, starting transfers between devices: 153 us -> none  [the longest x99 79.7 us: halo_axis(): from_next = lax.ppermute(low_part, axis_name, to_prev)]
    pallas_call x0 -> x1, Pallas kernels: none -> 140 us  [local_sweeps(): pl.pallas_call(functools.partial(kernel, omega_sweep.shape[0]), out_shape...]
    ppermute x198 -> x0, waiting for transfers between devices: 135 us -> none  [the longest x99 76.8 us: halo_axis(): from_prev = lax.ppermute(high_part, axis_name, to_next)]
    concatenate x66 -> x0, other arithmetic: 111 us -> none  [halo_axis(): return jnp.concatenate([from_prev, brick_in, from_next], axis=axis_dim)]
    ppermute x66 -> x0, local copies, waits for them, and re-layouts: 103 us -> none  [the longest x33 51.6 us: halo_axis(): from_prev = lax.ppermute(high_part, axis_name, to_next)]
    while x480 -> x0, local copies, waits for them, and re-layouts: 81.7 us -> none
    slice x167 -> x1, local copies, waits for them, and re-layouts: 65.8 us -> 2.54 us  [fold_in(): straight, mirrored = (brick[:, :, :NU], brick[:, :, NU:][:, :, ::-1])]
  transfers between devices with their start and end apart: 198 -> 1, of which waited for: 133 -> 1; matrix products, arithmetic and copies ran while one was open for 7% -> 0% of each run, Pallas kernels for 0% -> 0%
where the time goes in v1:
time: 214 us; the launch traced here: 213 us
  Pallas kernels  140 us (65%)
  local copies, waits for them, and re-layouts  46.9 us (22%)
  other arithmetic  15.6 us (7%)
  blocking collectives  4.24 us (2%)
  starting transfers between devices  3.67 us (2%)
  waiting for transfers between devices  2.62 us (1%)
    pallas_call x1, Pallas kernels, local_sweeps(): pl.pallas_call(functools.partial(kernel, omega_sweep.shape[0]), out_shape...  140 us
    unnamed x9, local copies, waits for them, and re-layouts  15.5 us
    another operation x7, local copies, waits for them, and re-layouts, local_sweeps(): u, f, k = fold_in(jnp.stack([u_brick, f_brick, kappa_brick]), gy)  12.7 us
    rev x1, local copies, waits for them, and re-layouts, fold_in(): straight, mirrored = (brick[:, :, :NU], brick[:, :, NU:][:, :, ::-1])  6.28 us
    all_to_all x1, other arithmetic, fold_in(): brick = lax.all_to_all(brick, 'gx', split_axis=3, concat_axis=1, tiled=True)  5.45 us
  transfers between devices with their start and end apart: 1, of which 1 were waited for; matrix products, arithmetic and copies ran while one was open for 0% of the time, Pallas kernels for 0%

profile of v1, /device:TPU:0, one launch (start us, length us, event | category | flops | bytes accessed | tf_op | source)
XLA Modules:
  0.0 213.3 jit_solution(12153608155929990206)
XLA Ops:
  0.0 3.1 %copy.30 = f32[32,64,64]{1,0,2:T(8,128)} copy(f32[32,64,64]{2,1,0:T(8,128)} %param.5) | data formatting | bytes 1048576 | tf_op args[0]
  3.1 3.0 %copy.31 = f32[32,64,64]{1,0,2:T(8,128)} copy(f32[32,64,64]{2,1,0:T(8,128)} %param.6) | data formatting | bytes 1048576 | tf_op args[1]
  6.1 1.8 copy.32
  7.9 2.3 %fusion.1 = f32[64,3,32,64]{3,2,1,0:T(8,128)S(1)} fusion(f32[1,32,64,64]{2,1,0,3:T(8,128)} %bitcast.44, f32[1,32,64,64]{2,1,0,3:T(8,128)} %bitcast.43, f32[1,32,64,64]{2,1,0,3:T(8,128)} %bitcast.42), kind=kLoop, calls=%fused_computation.8 | loop fusion | flops 786432 | bytes 3145728
  10.2 2.9 %reshape.15 = f32[2,1,196608]{2,1,0:T(1,128)} reshape(f32[64,3,32,64]{3,2,1,0:T(8,128)S(1)} %fusion.1) | data formatting | bytes 3145728
  13.1 3.7 %all-to-all-start = ((f32[2,1,196608]{2,1,0:T(1,128)}), f32[2,1,196608]{2,1,0:T(1,128)S(1)}, u32[]{:S(2)}, u32[]{:S(2)}) async-start(f32[2,1,196608]{2,1,0:T(1,128)} %reshape.15), calls=%async_computation | async-start | bytes 3145728 | tf_op jit(solution)/shard_map/all_to_all | solution.py:202
  16.8 2.6 %all-to-all-done = f32[2,1,196608]{2,1,0:T(1,128)S(1)} async-done(((f32[2,1,196608]{2,1,0:T(1,128)}), f32[2,1,196608]{2,1,0:T(1,128)S(1)}, u32[]{:S(2)}, u32[]{:S(2)}) %all-to-all-start) | async-done | bytes 1572896 | tf_op jit(solution)/shard_map/all_to_all | solution.py:202
  19.9 5.4 %reduce = f32[2,196608]{1,0:T(2,128)S(1)} reduce(f32[2,1,196608]{2,1,0:T(1,128)S(1)} %all-to-all-done, f32[]{:T(128)} %broadcast.3), dimensions={1}, to_apply=%all_to_all.26.reduce_sub_computation | reduce | bytes 3145732 | tf_op jit(solution)/shard_map/all_to_all | solution.py:202
  25.4 3.4 %reshape.16 = f32[64,3,32,64]{3,2,1,0:T(8,128)} reshape(f32[2,196608]{1,0:T(2,128)S(1)} %reduce) | data formatting | bytes 3145728
  28.8 3.7 %copy.34 = f32[3,2,32,64,32]{3,4,2,1,0:T(8,128)S(1)} copy(f32[3,2,32,64,32]{3,2,0,4,1:T(8,128)} %bitcast.35) | data formatting | bytes 3145728 | tf_op jit(solution)/shard_map/all_to_all | solution.py:202
  32.5 2.5 %slice.20 = f32[3,64,32,32]{2,3,1,0:T(8,128)} slice(f32[3,64,64,32]{2,3,1,0:T(8,128)S(1)} %bitcast.33), slice={[0:3], [0:64], [32:64], [0:32]} | slice | bytes 1572864 | tf_op jit(solution)/shard_map/slice | solution.py:203
  35.0 6.3 %rev.6 = f32[3,64,32,32]{2,3,1,0:T(8,128)} reverse(f32[3,64,32,32]{2,3,1,0:T(8,128)} %slice.20), dimensions={2} | reverse | bytes 1572864 | tf_op jit(solution)/shard_map/rev | solution.py:203
  41.3 2.7 %select_bitcast_fusion.1 = (f32[3,64,32,32,1]{2,3,1,0,4:T(8,128)S(1)}, f32[3,64,32,32,1]{2,3,1,0,4:T(8,128)S(1)}) fusion(f32[3,64,32,32]{2,3,1,0:T(8,128)} %rev.6, f32[3,64,64,32]{2,3,1,0:T(8,128)S(1)} %bitcast.34, pred[]{:T(512)S(6)} %eq.2), kind=kLoop, calls=%fused_computation.3 | loop fusion | flops 393216 | bytes 3145729 | tf_op jit(solution)/shard_map/stack | solution.py:206
  45.3 2.7 %fusion = (f32[1,32,32,64,2]{2,1,3,0,4:T(8,128)S(1)}, f32[1,32,32,64,2]{2,1,3,0,4:T(8,128)}, f32[1,32,32,64,2]{2,1,3,0,4:T(8,128)}) fusion(f32[3,32,32,64,2]{2,1,3,0,4:T(8,128)S(1)} %maximum_bitcast_fusion), kind=kLoop, calls=%fused_computation.7 | loop fusion | bytes 3145728 | tf_op jit(solution)/shard_map/unstack | solution.py:224
  48.1 2.1 copy.42.k_ref
  50.2 1.8 copy.38
  52.0 2.1 copy.41.f_ref
  54.1 1.8 copy.37
  55.9 2.1 copy.40.u_ref
  58.0 140.0 %shard_map.55 = f32[32,32,128]{2,1,0:T(8,128)} custom-call(f32[26]{0:T(128)} %w_ref.1, f32[32]{0:T(128)} %om_ref.1, f32[32,32,128]{2,1,0:T(8,128)} %copy.40.u_ref, f32[32,32,128]{2,1,0:T(8,128)} %copy.41.f_ref, f32[32,32,128]{2,1,0:T(8,128)} %copy.42.k_ref), custom_call_target="tpu_custom_call" | custom-call | tf_op jit(solution)/shard_map/pallas_call | solution.py:227
  198.1 2.9 %copy.43 = f32[32,32,128]{1,0,2:T(8,128)S(1)} copy(f32[32,32,128]{2,1,0:T(8,128)} %shard_map.55) | data formatting | bytes 1048576 | tf_op jit(solution)/shard_map/pallas_call | solution.py:227
  202.2 1.5 rev.7
  204.7 4.2 %all_to_all.36 = f32[2,1,65536]{2,1,0:T(1,128)S(1)} all-to-all(f32[2,1,65536]{2,1,0:T(1,128)S(1)} %reshape.17), channel_id=1, replica_groups=mesh['batch'=1,'gz'=2,'gy'=2,'gx'=2] {'gx'}, dimensions={0} | all-to-all | bytes 1048576 | tf_op jit(solution)/shard_map/all_to_all | solution.py:216
  208.9 2.3 %reduce.1 = f32[2,65536]{1,0:T(2,128)S(1)} reduce(f32[2,1,65536]{2,1,0:T(1,128)S(1)} %all_to_all.36, f32[]{:T(128)} %broadcast.3), dimensions={1}, to_apply=%all_to_all.30.reduce_sub_computation | reduce | bytes 1048580 | tf_op jit(solution)/shard_map/all_to_all | solution.py:216
  (11 shorter events, 6.3 us)
Async XLA Ops:
  0.0 6.1 %copy-start = (f32[32,64,64]{2,1,0:T(8,128)S(1)}, f32[32,64,64]{2,1,0:T(8,128)}, u32[]{:S(2)}) copy-start(f32[32,64,64]{2,1,0:T(8,128)} %param.7) | copy-start | bytes 1572868
  13.1 6.3 %all-to-all-start = ((f32[2,1,196608]{2,1,0:T(1,128)}), f32[2,1,196608]{2,1,0:T(1,128)S(1)}, u32[]{:S(2)}, u32[]{:S(2)}) async-start(f32[2,1,196608]{2,1,0:T(1,128)} %reshape.15), calls=%async_computation | async-start | bytes 3145728 | tf_op jit(solution)/shard_map/all_to_all | solution.py:202
